TPU v7x, 512 devices: a whole 4x4x16 slice. The times are simulated.
512 devices in a mesh: row: 16 (over z), col: 16 (over y, x), layer: 2 (over core).
Axes of the slice: x: 4, y: 4, z: 16, core: 2. Of those that a mesh axis runs over, the one named last changes fastest.
Arguments:
- ratings: bfloat16 [32768, 16384], P('row', ('col', 'layer')), may hold values from -6 to 6
- tile_mask: int32 [256, 128], P('row', ('col', 'layer')), may hold values 0 or 1
- tile_counts: int32 [256, 128], P('row', ('col', 'layer')), may hold values from 1 to 16384
- user_factor: float32 [256, 32768], P(('col', 'layer'), 'row'), may hold values from -1.5 to 1.5
- item_factor: float32 [256, 16384], P('row', ('col', 'layer')), may hold values from -1.5 to 1.5
Outputs:
- new_user: float32 [256, 32768], P(('col', 'layer'), 'row')
- new_item: float32 [256, 16384], P('row', ('col', 'layer'))
- loss_value: float32 [], replicated
- grad_norm: float32 [], replicated
All inputs are finite; a program needn't handle non-finite values. No bound on the sum of `tile_mask` on one device may be relied on, other than what follows from the above.
Results may differ from a plain program's by a relative error of at most 0.0049.
Values may be sent and summed in bfloat16 or wider, within the bound.
No kernel may reach another device: no remote copies, remote signals or barrier semaphores. Data moves between devices by JAX's collectives and lax.ppermute only.
A program may use at most 64 MiB of HBM per device.

v0:
```python
import jax
import jax.numpy as jnp
from jax import lax
from jax.experimental import pallas as pl
from jax.experimental.pallas import tpu as pltpu
from jax.sharding import Mesh
from jax.sharding import PartitionSpec as P

TILE = 128
LANES = 128
STRIPE = 512
SCATTER_FIRST, SCALARS_FIRST, CHIP_FIRST = 9, 8, 15
COL_LAYER = ("col_0", "col_1", "layer")
VMEM = pl.BlockSpec(memory_space=pltpu.VMEM)
SMEM = pl.BlockSpec(memory_space=pltpu.SMEM)
FAR = pl.BlockSpec(memory_space=pltpu.HBM)
GRANT = pltpu.CompilerParams(vmem_limit_bytes=16 * 2**20)
MOST_GRANT = pltpu.CompilerParams(vmem_limit_bytes=50 * 2**20)
WHOLE_GRANT = pltpu.CompilerParams(vmem_limit_bytes=60 * 2**20)

epsilon = 1e-12
trust_ratio = 0.2


def lower_body(user_ref, mask_ref, counts_ref, blocks_ref, limits_ref):
    user = user_ref[...].astype(jnp.bfloat16)
    blocks_ref[...] = jnp.broadcast_to(user[None], blocks_ref.shape)
    limits_ref[...] = jnp.where(mask_ref[...] == 1, counts_ref[...], 0)


def lowered_for_all(factor, mask, counts, devices):
    return pl.pallas_call(
        lower_body,
        in_specs=[VMEM] * 3,
        out_specs=[VMEM] * 2,
        out_shape=[
            jax.ShapeDtypeStruct((devices, *factor.shape), jnp.bfloat16),
            jax.ShapeDtypeStruct(mask.shape, jnp.int32),
        ],
        compiler_params=WHOLE_GRANT,
        name="lower",
    )(factor, mask, counts)


def residual_body(
    far_limits_ref, far_user_ref, far_item_ref, far_ratings_ref,
    scaled_ref, item_share_ref, error_ref,
    limits_ref, user_ref, item_ref, ratings_ref, total_ref, sems, ratings_sems,
):
    columns = ratings_ref.shape[1]
    starts = range(0, ratings_ref.shape[0], STRIPE)
    stripes = [pl.ds(start, STRIPE) for start in starts]
    rank = user_ref.shape[0]
    turn = CHIP_FIRST * rank // 16
    pairs = [
        (far_item_ref, item_ref),
        (far_limits_ref, limits_ref),
        (far_user_ref.at[pl.ds(0, rank - turn)], user_ref.at[pl.ds(turn, rank - turn)]),
        (far_user_ref.at[pl.ds(rank - turn, turn)], user_ref.at[pl.ds(0, turn)]),
    ]
    copies = [pltpu.make_async_copy(far, near, sems.at[at]) for at, (far, near) in enumerate(pairs)]
    ratings_copies = [
        pltpu.make_async_copy(far_ratings_ref.at[stripe], ratings_ref.at[stripe], ratings_sems.at[at])
        for at, stripe in enumerate(stripes)
    ]
    for copy in copies + ratings_copies:
        copy.start()
    for copy in copies:
        copy.wait()
    item = item_ref[...]
    side = (TILE, TILE)
    position = lax.broadcasted_iota(jnp.int32, side, 0) * TILE + lax.broadcasted_iota(jnp.int32, side, 1)

    def predicted_of(at):
        user = user_ref[:, stripes[at]]
        return lax.dot_general(user, item, (((0,), (0,)), ((), ())), preferred_element_type=jnp.float32)

    def add_share(at):
        share = jnp.dot(user_ref[:, stripes[at]], scaled_ref[stripes[at]], preferred_element_type=jnp.float32)
        if at > 0:
            share = share + total_ref[...]
        if at + 1 < len(stripes):
            total_ref[...] = share
        else:
            blocks = share.astype(jnp.bfloat16).reshape(item_share_ref.shape)
            first = SCATTER_FIRST * blocks.shape[0] // 16
            item_share_ref[...] = jnp.concatenate([blocks[first:], blocks[:first]]) if first else blocks

    predicted = predicted_of(0)
    errors = [jnp.zeros((8, TILE), jnp.float32)] * (columns // TILE)
    for at, start in enumerate(starts):
        ratings_copies[at].wait()
        following = predicted_of(at + 1) if at + 1 < len(stripes) else None
        for row in range(0, STRIPE, TILE):
            for column in range(0, columns, TILE):
                limit = limits_ref[column // TILE, (start + row) // TILE]
                rows, cols = pl.ds(start + row, TILE), pl.ds(column, TILE)
                rating = ratings_ref[rows, cols].astype(jnp.float32)
                difference = predicted[row : row + TILE, column : column + TILE] - rating
                residual = jnp.where(position < limit, difference, 0.0)
                scaled_ref[rows, cols] = residual.astype(jnp.bfloat16)
                error = (residual * residual).reshape(TILE // 8, 8, TILE).sum(axis=0)
                errors[column // TILE] = errors[column // TILE] + error
        if at > 0:
            add_share(at - 1)
        predicted = following
    add_share(len(stripes) - 1)
    error_ref[...] = jnp.concatenate(errors, axis=1)


def residual_of(limits, user, item, ratings, devices):
    rank, columns = item.shape
    flops = 4 * rank * ratings.size
    return pl.pallas_call(
        residual_body,
        in_specs=[FAR] * 4,
        out_specs=[VMEM] * 3,
        out_shape=[
            jax.ShapeDtypeStruct(ratings.shape, jnp.bfloat16),
            jax.ShapeDtypeStruct((devices, rank // devices, columns), jnp.bfloat16),
            jax.ShapeDtypeStruct((8, columns), jnp.float32),
        ],
        scratch_shapes=[
            pltpu.SMEM(limits.shape, jnp.int32),
            pltpu.VMEM(user.shape, jnp.bfloat16),
            pltpu.VMEM(item.shape, jnp.bfloat16),
            pltpu.VMEM(ratings.shape, jnp.bfloat16),
            pltpu.VMEM((rank, columns), jnp.float32),
            pltpu.SemaphoreType.DMA((4,)),
            pltpu.SemaphoreType.DMA((ratings.shape[0] // STRIPE,)),
        ],
        cost_estimate=pl.CostEstimate(flops=flops, bytes_accessed=4 * ratings.size, transcendentals=0),
        compiler_params=MOST_GRANT,
        name="residual",
    )(limits, user, item, ratings)


def user_share_body(layer_ref, item_ref, scaled_ref, mine_ref, other_ref):
    chips, height, _ = mine_ref.shape
    item = item_ref[...]
    first = layer_ref[0] == 0
    for start in range(0, scaled_ref.shape[0], STRIPE):
        stripe = pl.ds(start, STRIPE)
        share = lax.dot_general(item, scaled_ref[stripe], (((1,), (1,)), ((), ())), preferred_element_type=jnp.float32)
        share = share.reshape(chips, 2, height, STRIPE)
        for at in range(chips):
            even, odd = share[at, 0], share[at, 1]
            chip = (at - CHIP_FIRST * chips // 16) % chips
            mine_ref[chip, :, stripe] = jnp.where(first, even, odd).astype(jnp.bfloat16)
            other_ref[chip, :, stripe] = jnp.where(first, odd, even).astype(jnp.bfloat16)


def user_share_of(layer, item, scaled, height):
    shape = jax.ShapeDtypeStruct((item.shape[0] // height // 2, height, scaled.shape[0]), jnp.bfloat16)
    return pl.pallas_call(
        user_share_body,
        in_specs=[SMEM, VMEM, VMEM],
        out_specs=[VMEM, VMEM],
        out_shape=[shape, shape],
        cost_estimate=pl.CostEstimate(flops=2 * item.shape[0] * scaled.size, bytes_accessed=0, transcendentals=0),
        compiler_params=GRANT,
        name="user_share",
    )(layer, item, scaled)


def halves_body(mine_ref, arrived_ref, total_ref):
    total_ref[...] = (mine_ref[...].astype(jnp.float32) + arrived_ref[...].astype(jnp.float32)).astype(jnp.bfloat16)


def halves_summed(mine, arrived):
    return pl.pallas_call(
        halves_body,
        in_specs=[VMEM, VMEM],
        out_specs=VMEM,
        out_shape=jax.ShapeDtypeStruct(mine.shape, jnp.bfloat16),
        compiler_params=GRANT,
        name="halves",
    )(mine, arrived)


def summed(blocks_ref):
    total = blocks_ref[0].astype(jnp.float32)
    for i in range(1, blocks_ref.shape[0]):
        total = total + blocks_ref[i].astype(jnp.float32)
    return total


def item_raw_body(limits_ref, arrived_ref, user_ref, item_ref, error_ref, raw_ref, sums_ref):
    raw = summed(arrived_ref)
    raw_ref[...] = raw
    user, item = user_ref[...], item_ref[...]
    lane = lax.broadcasted_iota(jnp.int32, sums_ref.shape, 1)
    sums = jnp.zeros(sums_ref.shape, jnp.float32)
    for at, value in enumerate(
        (
            jnp.sum(limits_ref[...].astype(jnp.float32)),
            jnp.sum(user * user) + jnp.sum(item * item),
            jnp.sum(error_ref[...]),
            jnp.sum(raw * raw),
        )
    ):
        sums = jnp.where(lane == at, value, sums)
    sums_ref[...] = sums


def item_raw_of(limits, arrived, user_factor, item_factor, error):
    return pl.pallas_call(
        item_raw_body,
        in_specs=[VMEM] * 5,
        out_specs=[VMEM, VMEM],
        out_shape=[
            jax.ShapeDtypeStruct(arrived.shape[1:], jnp.float32),
            jax.ShapeDtypeStruct((1, LANES), jnp.float32),
        ],
        compiler_params=GRANT,
        name="item_raw",
    )(limits, arrived, user_factor, item_factor, error)


def user_raw_body(arrived_ref, sums_ref, raw_ref, packed_ref):
    raw = summed(arrived_ref)
    raw_ref[...] = raw
    lane = lax.broadcasted_iota(jnp.int32, sums_ref.shape, 1)
    sums = sums_ref[...] + jnp.where(lane == 3, jnp.sum(raw * raw), 0.0)
    packed_ref[...] = jnp.broadcast_to(sums[None], packed_ref.shape)


def user_raw_of(arrived, sums, devices):
    return pl.pallas_call(
        user_raw_body,
        in_specs=[VMEM, VMEM],
        out_specs=[VMEM, VMEM],
        out_shape=[
            jax.ShapeDtypeStruct(arrived.shape[1:], jnp.float32),
            jax.ShapeDtypeStruct((devices, *sums.shape), jnp.float32),
        ],
        compiler_params=GRANT,
        name="user_raw",
    )(arrived, sums)


def packed_again_body(arrived_ref, packed_ref):
    packed_ref[...] = jnp.broadcast_to(summed(arrived_ref)[None], packed_ref.shape)


def packed_again(arrived, devices):
    return pl.pallas_call(
        packed_again_body,
        in_specs=[VMEM],
        out_specs=VMEM,
        out_shape=jax.ShapeDtypeStruct((devices, *arrived.shape[1:]), jnp.float32),
        compiler_params=GRANT,
        name="packed_again",
    )(arrived)


def step_body(arrived_ref, user_ref, item_ref, raw_user_ref, raw_item_ref, new_user_ref, new_item_ref, loss_ref, norm_ref):
    sums = summed(arrived_ref)
    lane = lax.broadcasted_iota(jnp.int32, sums.shape, 1)

    def lane_at(at):
        return jnp.sum(jnp.where(lane == at, sums, 0.0), axis=1, keepdims=True)

    observed_total = jnp.maximum(lane_at(0), 1.0)
    scale = 2.0 / observed_total
    grad_norm = scale * jnp.sqrt(lane_at(3) + epsilon)
    step_size = trust_ratio * jnp.sqrt(lane_at(1) + epsilon) / grad_norm * scale
    new_user_ref[...] = user_ref[...] - step_size * raw_user_ref[...]
    new_item_ref[...] = item_ref[...] - step_size * raw_item_ref[...]
    loss_ref[0, 0] = jnp.sum(lane_at(2) / observed_total)
    norm_ref[0, 0] = jnp.sum(grad_norm)


def stepped(arrived, user_factor, item_factor, raw_user, raw_item):
    return pl.pallas_call(
        step_body,
        in_specs=[VMEM] * 5,
        out_specs=[VMEM, VMEM, SMEM, SMEM],
        out_shape=[
            jax.ShapeDtypeStruct(user_factor.shape, jnp.float32),
            jax.ShapeDtypeStruct(item_factor.shape, jnp.float32),
            jax.ShapeDtypeStruct((1, 1), jnp.float32),
            jax.ShapeDtypeStruct((1, 1), jnp.float32),
        ],
        compiler_params=GRANT,
        name="step",
    )(arrived, user_factor, item_factor, raw_user, raw_item)


def exchanged(blocks, axis, groups=None):
    return lax.all_to_all(blocks, axis, 0, 0, tiled=True, axis_index_groups=groups)


def listed_from(first, count):
    return [[(first + i) % count for i in range(count)]]


def shifted(array, axis, by):
    count = lax.axis_size(axis)
    return lax.ppermute(array, axis, [(i, (i + by) % count) for i in range(count)])


def body(ratings, tile_mask, tile_counts, user_factor, item_factor):
    rows, height = lax.axis_size("row"), user_factor.shape[0]
    devices, chips = lax.axis_size(COL_LAYER), lax.axis_size(("col_0", "col_1"))
    scatter_list, scalars_list = (listed_from(first * rows // 16, rows) for first in (SCATTER_FIRST, SCALARS_FIRST))
    chips_list, devices_list = (listed_from(CHIP_FIRST * count // 16, count) for count in (chips, devices))
    layer = lax.axis_index("layer").astype(jnp.int32)[None]
    user_blocks, limits = lowered_for_all(user_factor, tile_mask.T, tile_counts.T, devices)
    user = exchanged(user_blocks, COL_LAYER, devices_list).reshape(-1, user_factor.shape[1])
    item = lax.all_gather(item_factor.astype(jnp.bfloat16), "row", axis=0, tiled=True)
    scaled, item_share, error = residual_of(limits, user, item, ratings, rows)
    item_arrived = exchanged(item_share, "row", scatter_list)
    my_share, other_share = user_share_of(layer, item, scaled, height)
    partner_share = shifted(other_share, "layer", 1)
    halves = halves_summed(my_share, partner_share)
    user_arrived = exchanged(halves, ("col_0", "col_1"), chips_list)
    raw_item, sums = item_raw_of(limits, item_arrived, user_factor, item_factor, error)
    raw_user, packed = user_raw_of(user_arrived, sums, rows)
    packed = exchanged(packed, "row", scalars_list)
    packed = packed_again(packed, devices)
    packed = exchanged(packed, COL_LAYER, devices_list)
    new_user, new_item, loss_value, grad_norm = stepped(packed, user_factor, item_factor, raw_user, raw_item)
    return (new_user, new_item, loss_value.reshape(()), grad_norm.reshape(()))


def solution(mesh):
    finer = Mesh(
        mesh.devices.reshape(mesh.shape["row"], 4, 4, mesh.shape["layer"]),
        ("row", "col_0", "col_1", "layer"),
    )
    return jax.shard_map(
        body,
        mesh=finer,
        in_specs=(
            P("row", COL_LAYER),
            P("row", COL_LAYER),
            P("row", COL_LAYER),
            P(COL_LAYER, "row"),
            P("row", COL_LAYER),
        ),
        out_specs=(P(COL_LAYER, "row"), P("row", COL_LAYER), P(), P()),
        check_vma=False,
    )
```

profile of v0, /device:TPU:1, one launch (start us, length us, event | category | flops | bytes accessed | tf_op | source)
XLA Modules:
  0.0 114.0 jit_solution(6257593153422115782)
XLA Ops:
  0.6 0.0 copy-start.1
  0.6 2.0 %lower.1 = (bf16[32,8,2048]{2,1,0:T(8,128)(2,1)}, s32[4,16]{1,0:T(4,128)}) custom-call(f32[8,2048]{1,0:T(8,128)} %user_ref.5, s32[4,16]{1,0:T(4,128)} %bitcast.7, s32[4,16]{1,0:T(4,128)} %bitcast.8), custom_call_target="tpu_custom_call" | custom-call | tf_op jit(solution)/shard_map/lower/pallas_call | solution.py:32
  2.6 0.0 copy-start.3
  2.6 13.4 %all-to-all-start = ((bf16[32,8,2048]{2,1,0:T(8,128)(2,1)}), bf16[32,8,2048]{2,1,0:T(8,128)(2,1)S(1)}, u32[]{:S(2)}, u32[]{:S(2)}) async-start(bf16[32,8,2048]{2,1,0:T(8,128)(2,1)} %get-tuple-element.20), calls=%async_computation | async-start | bytes 2097152 | tf_op jit(solution)/shard_map/all_to_all | solution.py:291
  16.0 0.0 copy-done.1
  16.0 27.1 %all_gather.3.far_item_ref.item_ref = bf16[256,512]{1,0:T(8,128)(2,1)S(1)} all-gather(bf16[16,512]{1,0:T(8,128)(2,1)S(1)} %convert_element_type.3), channel_id=1, replica_groups=mesh['row'=16,'col_0'=4,'col_1'=4,'layer'=2] {'row'}, dimensions={0}, use_global_device_ids=true | all-gather | bytes 278528 | tf_op jit(solution)/shard_map/all_gather | solution.py:311
  43.1 0.0 all-to-all-done
  43.1 0.0 copy-done.3
  43.1 3.9 %residual.1 = (bf16[2048,512]{1,0:T(8,128)(2,1)S(1)}, bf16[16,16,512]{2,1,0:T(8,128)(2,1)S(1)}, f32[8,512]{1,0:T(8,128)S(1)}) custom-call(s32[4,16]{1,0:T(4,128)S(1)} %copy-done.3, bf16[256,2048]{1,0:T(8,128)(2,1)S(1)} %bitcast.6, bf16[256,512]{1,0:T(8,128)(2,1)S(1)} %all_gather.3.far_item_ref.item_ref, bf16[2048,512]{1,0:T(8,128)(2,1)} %far_ratings_ref.1), custom_call_target="tpu_custom_call" | custom-call | flops 1073741824 | bytes 4194304 | tf_op jit(solution)/shard_map/residual/pallas_call | solution.py:114
  47.0 0.0 copy-start.2
  47.0 0.7 copy-done.2
  47.7 10.6 %all-to-all-start.2 = ((bf16[16,16,512]{2,1,0:T(8,128)(2,1)}), bf16[16,16,512]{2,1,0:T(8,128)(2,1)S(1)}, u32[]{:S(2)}, u32[]{:S(2)}) async-start(bf16[16,16,512]{2,1,0:T(8,128)(2,1)} %copy-done.2), calls=%async_computation.2 | async-start | bytes 524288 | tf_op jit(solution)/shard_map/all_to_all | solution.py:291
  58.3 0.0 copy-start
  58.3 0.7 user_share.1
  59.1 9.2 %collective-permute-start = (bf16[16,8,2048]{2,1,0:T(8,128)(2,1)S(1)}, bf16[16,8,2048]{2,1,0:T(8,128)(2,1)S(1)}, u32[]{:S(2)}, u32[]{:S(2)}) collective-permute-start(bf16[16,8,2048]{2,1,0:T(8,128)(2,1)S(1)} %get-tuple-element.23), channel_id=1, source_target_pairs={{0,1},{1,0},{2,3},{3,2},{4,5},{5,4},{6,7},{7,6},{8,9},{9,8},{10,11... | collective-permute-start | bytes 1572872 | tf_op jit(solution)/shard_map/ppermute | solution.py:300
  68.3 1.5 %collective-permute-done.arrived_ref = bf16[16,8,2048]{2,1,0:T(8,128)(2,1)S(1)} collective-permute-done((bf16[16,8,2048]{2,1,0:T(8,128)(2,1)S(1)}, bf16[16,8,2048]{2,1,0:T(8,128)(2,1)S(1)}, u32[]{:S(2)}, u32[]{:S(2)}) %collective-permute-start) | collective-permute-done | bytes 524320 | tf_op jit(solution)/shard_map/ppermute | solution.py:300
  69.8 0.9 halves.1
  70.7 0.0 all-to-all-done.2.arrived_ref
  70.7 6.7 %all-to-all-start.1 = ((bf16[16,8,2048]{2,1,0:T(8,128)(2,1)}), bf16[16,8,2048]{2,1,0:T(8,128)(2,1)S(1)}, u32[]{:S(2)}, u32[]{:S(2)}) async-start(bf16[16,8,2048]{2,1,0:T(8,128)(2,1)} %halves.1), calls=%async_computation.1 | async-start | bytes 1048576 | tf_op jit(solution)/shard_map/all_to_all | solution.py:291
  77.4 0.0 copy-done
  77.5 0.2 item_raw.1
  77.6 5.0 %all-to-all-done.1.arrived_ref = bf16[16,8,2048]{2,1,0:T(8,128)(2,1)S(1)} async-done(((bf16[16,8,2048]{2,1,0:T(8,128)(2,1)}), bf16[16,8,2048]{2,1,0:T(8,128)(2,1)S(1)}, u32[]{:S(2)}, u32[]{:S(2)}) %all-to-all-start.1) | async-done | bytes 524320 | tf_op jit(solution)/shard_map/all_to_all | solution.py:291
  82.6 0.2 user_raw.1
  82.9 13.2 %all_to_all.25.arrived_ref = f32[16,1,128]{2,1,0:T(1,128)S(1)} all-to-all(f32[16,1,128]{2,1,0:T(1,128)S(1)} %get-tuple-element.27), channel_id=1, replica_groups={{256,288,320,352,384,416,448,480,0,32,64,96,128,160,192,224},{257,289,3..., dimensions={0} | all-to-all | bytes 16384 | tf_op jit(solution)/shard_map/all_to_all | solution.py:291
  96.1 17.1 %all_to_all.26.arrived_ref = f32[32,1,128]{2,1,0:T(1,128)S(1)} all-to-all(f32[32,1,128]{2,1,0:T(1,128)S(1)} %packed_again.1), channel_id=1, replica_groups={{30,31,0,1,2,3,4,5,6,7,8,9,10,11,12,13,14,15,16,17,18,19,20,21,22,23,24..., dimensions={0} | all-to-all | bytes 32768 | tf_op jit(solution)/shard_map/all_to_all | solution.py:291
  113.2 0.8 step.1
  (2 shorter events, 0.0 us)
Async XLA Ops:
  0.6 15.3 %copy-start.1 = (f32[16,512]{1,0:T(8,128)S(1)}, f32[16,512]{1,0:T(8,128)}, u32[]{:S(2)}) copy-start(f32[16,512]{1,0:T(8,128)} %item_ref.3) | copy-start | bytes 98308
  2.6 40.5 %copy-start.3 = (s32[4,16]{1,0:T(4,128)S(1)}, s32[4,16]{1,0:T(4,128)}, u32[]{:S(2)}) copy-start(s32[4,16]{1,0:T(4,128)} %get-tuple-element.19.far_limits_ref.limits_ref) | copy-start | bytes 772
  2.6 40.5 %all-to-all-start = ((bf16[32,8,2048]{2,1,0:T(8,128)(2,1)}), bf16[32,8,2048]{2,1,0:T(8,128)(2,1)S(1)}, u32[]{:S(2)}, u32[]{:S(2)}) async-start(bf16[32,8,2048]{2,1,0:T(8,128)(2,1)} %get-tuple-element.20), calls=%async_computation | async-start | bytes 2097152 | tf_op jit(solution)/shard_map/all_to_all | solution.py:291
  47.0 0.7 copy-start.2
  47.7 23.0 %all-to-all-start.2 = ((bf16[16,16,512]{2,1,0:T(8,128)(2,1)}), bf16[16,16,512]{2,1,0:T(8,128)(2,1)S(1)}, u32[]{:S(2)}, u32[]{:S(2)}) async-start(bf16[16,16,512]{2,1,0:T(8,128)(2,1)} %copy-done.2), calls=%async_computation.2 | async-start | bytes 524288 | tf_op jit(solution)/shard_map/all_to_all | solution.py:291
  58.3 19.1 %copy-start = (f32[8,2048]{1,0:T(8,128)S(1)}, f32[8,2048]{1,0:T(8,128)}, u32[]{:S(2)}) copy-start(f32[8,2048]{1,0:T(8,128)} %user_ref.5) | copy-start | bytes 196612
  59.1 10.8 %collective-permute-start = (bf16[16,8,2048]{2,1,0:T(8,128)(2,1)S(1)}, bf16[16,8,2048]{2,1,0:T(8,128)(2,1)S(1)}, u32[]{:S(2)}, u32[]{:S(2)}) collective-permute-start(bf16[16,8,2048]{2,1,0:T(8,128)(2,1)S(1)} %get-tuple-element.23), channel_id=1, source_target_pairs={{0,1},{1,0},{2,3},{3,2},{4,5},{5,4},{6,7},{7,6},{8,9},{9,8},{10,11... | collective-permute-start | bytes 1572872 | tf_op jit(solution)/shard_map/ppermute | solution.py:300
  70.7 11.9 %all-to-all-start.1 = ((bf16[16,8,2048]{2,1,0:T(8,128)(2,1)}), bf16[16,8,2048]{2,1,0:T(8,128)(2,1)S(1)}, u32[]{:S(2)}, u32[]{:S(2)}) async-start(bf16[16,8,2048]{2,1,0:T(8,128)(2,1)} %halves.1), calls=%async_computation.1 | async-start | bytes 1048576 | tf_op jit(solution)/shard_map/all_to_all | solution.py:291
where the time goes:
time: 115 us; the launch traced here: 114 us
  blocking collectives  57.4 us (50%)
  starting transfers between devices  39.9 us (35%)
  Pallas kernels  8.71 us (8%)
  waiting for transfers between devices  6.53 us (6%)
    all_to_all x3, starting transfers between devices, exchanged(): lax.all_to_all(blocks, axis, 0, 0, tiled=True, axis_index_groups=groups)  30.6 us
    all_to_all x2, blocking collectives, exchanged(): lax.all_to_all(blocks, axis, 0, 0, tiled=True, axis_index_groups=groups)  30.3 us
    all_gather x1, blocking collectives, body(): lax.all_gather(item_factor.astype(jnp.bfloat16), 'row', axis=0, tiled=True)  27.1 us
    ppermute x1, starting transfers between devices, shifted(): lax.ppermute(array, axis, [(i, (i + by) % count) for i in range(count)])  9.24 us
    all_to_all x3, waiting for transfers between devices, exchanged(): lax.all_to_all(blocks, axis, 0, 0, tiled=True, axis_index_groups=groups)  5.01 us
    pallas_call x1, Pallas kernels, residual_of(): pl.pallas_call(residual_body, in_specs=[FAR] * 4, out_specs=[VMEM] * 3, o...  3.91 us
  transfers between devices with their start and end apart: 4, of which 2 were waited for; matrix products, arithmetic and copies ran while one was open for 0% of the time, Pallas kernels for 2%

commit v1 on v0

--- a/solution.py
+++ b/solution.py
@@ -9,7 +9,7 @@
 TILE = 128
 LANES = 128
 STRIPE = 512
-SCATTER_FIRST, SCALARS_FIRST, CHIP_FIRST = 9, 8, 15
+SCATTER_FIRST, SCALARS_FIRST, CHIP_FIRST = 8, 8, 15
 COL_LAYER = ("col_0", "col_1", "layer")
 VMEM = pl.BlockSpec(memory_space=pltpu.VMEM)
 SMEM = pl.BlockSpec(memory_space=pltpu.SMEM)
@@ -316,10 +316,10 @@
     halves = halves_summed(my_share, partner_share)
     user_arrived = exchanged(halves, ("col_0", "col_1"), chips_list)
     raw_item, sums = item_raw_of(limits, item_arrived, user_factor, item_factor, error)
-    raw_user, packed = user_raw_of(user_arrived, sums, rows)
+    raw_user, packed = user_raw_of(user_arrived, sums, devices)
+    packed = exchanged(packed, COL_LAYER, devices_list)
+    packed = packed_again(packed, rows)
     packed = exchanged(packed, "row", scalars_list)
-    packed = packed_again(packed, devices)
-    packed = exchanged(packed, COL_LAYER, devices_list)
     new_user, new_item, loss_value, grad_norm = stepped(packed, user_factor, item_factor, raw_user, raw_item)
     return (new_user, new_item, loss_value.reshape(()), grad_norm.reshape(()))
 

time: 115 us -> 113 us (0.983)
  blocking collectives: 57.4 us -> 54.7 us
    all_to_all x2, blocking collectives: 30.3 us -> 27.6 us  [exchanged(): lax.all_to_all(blocks, axis, 0, 0, tiled=True, axis_index_groups=groups)]
where the time goes in v1:
time: 113 us
  blocking collectives  54.7 us (48%)
  starting transfers between devices  40.8 us (36%)
  Pallas kernels  8.71 us (8%)
  waiting for transfers between devices  6.88 us (6%)
    all_to_all x3, starting transfers between devices, exchanged(): lax.all_to_all(blocks, axis, 0, 0, tiled=True, axis_index_groups=groups)  31.5 us
    all_to_all x2, blocking collectives, exchanged(): lax.all_to_all(blocks, axis, 0, 0, tiled=True, axis_index_groups=groups)  27.6 us
    all_gather x1, blocking collectives, body(): lax.all_gather(item_factor.astype(jnp.bfloat16), 'row', axis=0, tiled=True)  27.1 us
    ppermute x1, starting transfers between devices, shifted(): lax.ppermute(array, axis, [(i, (i + by) % count) for i in range(count)])  9.24 us
    all_to_all x3, waiting for transfers between devices, exchanged(): lax.all_to_all(blocks, axis, 0, 0, tiled=True, axis_index_groups=groups)  5.36 us
    pallas_call x1, Pallas kernels, residual_of(): pl.pallas_call(residual_body, in_specs=[FAR] * 4, out_specs=[VMEM] * 3, o...  3.91 us
  transfers between devices with their start and end apart: 4, of which 2 were waited for; matrix products, arithmetic and copies ran while one was open for 0% of the time, Pallas kernels for 2%

profile of v1, /device:TPU:1, one launch (start us, length us, event | category | flops | bytes accessed | tf_op | source)
XLA Modules:
  0.0 112.5 jit_solution(15373996261359563005)
XLA Ops:
  0.6 0.0 copy-start.1
  0.6 2.0 %lower.1 = (bf16[32,8,2048]{2,1,0:T(8,128)(2,1)}, s32[4,16]{1,0:T(4,128)}) custom-call(f32[8,2048]{1,0:T(8,128)} %user_ref.5, s32[4,16]{1,0:T(4,128)} %bitcast.7, s32[4,16]{1,0:T(4,128)} %bitcast.8), custom_call_target="tpu_custom_call" | custom-call | tf_op jit(solution)/shard_map/lower/pallas_call | solution.py:32
  2.6 0.0 copy-start.3
  2.6 13.4 %all-to-all-start = ((bf16[32,8,2048]{2,1,0:T(8,128)(2,1)}), bf16[32,8,2048]{2,1,0:T(8,128)(2,1)S(1)}, u32[]{:S(2)}, u32[]{:S(2)}) async-start(bf16[32,8,2048]{2,1,0:T(8,128)(2,1)} %get-tuple-element.20), calls=%async_computation | async-start | bytes 2097152 | tf_op jit(solution)/shard_map/all_to_all | solution.py:291
  16.0 0.0 copy-done.1
  16.0 27.1 %all_gather.3.far_item_ref.item_ref = bf16[256,512]{1,0:T(8,128)(2,1)S(1)} all-gather(bf16[16,512]{1,0:T(8,128)(2,1)S(1)} %convert_element_type.3), channel_id=1, replica_groups=mesh['row'=16,'col_0'=4,'col_1'=4,'layer'=2] {'row'}, dimensions={0}, use_global_device_ids=true | all-gather | bytes 278528 | tf_op jit(solution)/shard_map/all_gather | solution.py:311
  43.1 0.0 all-to-all-done
  43.1 0.0 copy-done.3
  43.1 3.9 %residual.1 = (bf16[2048,512]{1,0:T(8,128)(2,1)S(1)}, bf16[16,16,512]{2,1,0:T(8,128)(2,1)S(1)}, f32[8,512]{1,0:T(8,128)S(1)}) custom-call(s32[4,16]{1,0:T(4,128)S(1)} %copy-done.3, bf16[256,2048]{1,0:T(8,128)(2,1)S(1)} %bitcast.6, bf16[256,512]{1,0:T(8,128)(2,1)S(1)} %all_gather.3.far_item_ref.item_ref, bf16[2048,512]{1,0:T(8,128)(2,1)} %far_ratings_ref.1), custom_call_target="tpu_custom_call" | custom-call | flops 1073741824 | bytes 4194304 | tf_op jit(solution)/shard_map/residual/pallas_call | solution.py:114
  47.0 0.0 copy-start.2
  47.0 0.7 copy-done.2
  47.7 11.5 %all-to-all-start.2 = ((bf16[16,16,512]{2,1,0:T(8,128)(2,1)}), bf16[16,16,512]{2,1,0:T(8,128)(2,1)S(1)}, u32[]{:S(2)}, u32[]{:S(2)}) async-start(bf16[16,16,512]{2,1,0:T(8,128)(2,1)} %copy-done.2), calls=%async_computation.2 | async-start | bytes 524288 | tf_op jit(solution)/shard_map/all_to_all | solution.py:291
  59.2 0.0 copy-start
  59.2 0.7 user_share.1
  60.0 9.2 %collective-permute-start = (bf16[16,8,2048]{2,1,0:T(8,128)(2,1)S(1)}, bf16[16,8,2048]{2,1,0:T(8,128)(2,1)S(1)}, u32[]{:S(2)}, u32[]{:S(2)}) collective-permute-start(bf16[16,8,2048]{2,1,0:T(8,128)(2,1)S(1)} %get-tuple-element.23), channel_id=1, source_target_pairs={{0,1},{1,0},{2,3},{3,2},{4,5},{5,4},{6,7},{7,6},{8,9},{9,8},{10,11... | collective-permute-start | bytes 1572872 | tf_op jit(solution)/shard_map/ppermute | solution.py:300
  69.2 1.5 %collective-permute-done.arrived_ref = bf16[16,8,2048]{2,1,0:T(8,128)(2,1)S(1)} collective-permute-done((bf16[16,8,2048]{2,1,0:T(8,128)(2,1)S(1)}, bf16[16,8,2048]{2,1,0:T(8,128)(2,1)S(1)}, u32[]{:S(2)}, u32[]{:S(2)}) %collective-permute-start) | collective-permute-done | bytes 524320 | tf_op jit(solution)/shard_map/ppermute | solution.py:300
  70.7 0.9 halves.1
  71.6 0.0 all-to-all-done.2.arrived_ref
  71.6 6.7 %all-to-all-start.1 = ((bf16[16,8,2048]{2,1,0:T(8,128)(2,1)}), bf16[16,8,2048]{2,1,0:T(8,128)(2,1)S(1)}, u32[]{:S(2)}, u32[]{:S(2)}) async-start(bf16[16,8,2048]{2,1,0:T(8,128)(2,1)} %halves.1), calls=%async_computation.1 | async-start | bytes 1048576 | tf_op jit(solution)/shard_map/all_to_all | solution.py:291
  78.3 0.0 copy-done
  78.4 0.2 item_raw.1
  78.5 5.4 %all-to-all-done.1.arrived_ref = bf16[16,8,2048]{2,1,0:T(8,128)(2,1)S(1)} async-done(((bf16[16,8,2048]{2,1,0:T(8,128)(2,1)}), bf16[16,8,2048]{2,1,0:T(8,128)(2,1)S(1)}, u32[]{:S(2)}, u32[]{:S(2)}) %all-to-all-start.1) | async-done | bytes 524320 | tf_op jit(solution)/shard_map/all_to_all | solution.py:291
  83.9 0.2 user_raw.1
  84.1 14.7 %all_to_all.25.arrived_ref = f32[32,1,128]{2,1,0:T(1,128)S(1)} all-to-all(f32[32,1,128]{2,1,0:T(1,128)S(1)} %get-tuple-element.27), channel_id=1, replica_groups={{30,31,0,1,2,3,4,5,6,7,8,9,10,11,12,13,14,15,16,17,18,19,20,21,22,23,24..., dimensions={0} | all-to-all | bytes 32768 | tf_op jit(solution)/shard_map/all_to_all | solution.py:291
  98.9 12.9 %all_to_all.26.arrived_ref = f32[16,1,128]{2,1,0:T(1,128)S(1)} all-to-all(f32[16,1,128]{2,1,0:T(1,128)S(1)} %packed_again.1), channel_id=1, replica_groups={{256,288,320,352,384,416,448,480,0,32,64,96,128,160,192,224},{257,289,3..., dimensions={0} | all-to-all | bytes 16384 | tf_op jit(solution)/shard_map/all_to_all | solution.py:291
  111.8 0.8 step.1
  (2 shorter events, 0.0 us)
Async XLA Ops:
  0.6 15.3 %copy-start.1 = (f32[16,512]{1,0:T(8,128)S(1)}, f32[16,512]{1,0:T(8,128)}, u32[]{:S(2)}) copy-start(f32[16,512]{1,0:T(8,128)} %item_ref.3) | copy-start | bytes 98308
  2.6 40.5 %copy-start.3 = (s32[4,16]{1,0:T(4,128)S(1)}, s32[4,16]{1,0:T(4,128)}, u32[]{:S(2)}) copy-start(s32[4,16]{1,0:T(4,128)} %get-tuple-element.19.far_limits_ref.limits_ref) | copy-start | bytes 772
  2.6 40.5 %all-to-all-start = ((bf16[32,8,2048]{2,1,0:T(8,128)(2,1)}), bf16[32,8,2048]{2,1,0:T(8,128)(2,1)S(1)}, u32[]{:S(2)}, u32[]{:S(2)}) async-start(bf16[32,8,2048]{2,1,0:T(8,128)(2,1)} %get-tuple-element.20), calls=%async_computation | async-start | bytes 2097152 | tf_op jit(solution)/shard_map/all_to_all | solution.py:291
  47.0 0.7 copy-start.2
  47.7 23.9 %all-to-all-start.2 = ((bf16[16,16,512]{2,1,0:T(8,128)(2,1)}), bf16[16,16,512]{2,1,0:T(8,128)(2,1)S(1)}, u32[]{:S(2)}, u32[]{:S(2)}) async-start(bf16[16,16,512]{2,1,0:T(8,128)(2,1)} %copy-done.2), calls=%async_computation.2 | async-start | bytes 524288 | tf_op jit(solution)/shard_map/all_to_all | solution.py:291
  59.2 19.1 %copy-start = (f32[8,2048]{1,0:T(8,128)S(1)}, f32[8,2048]{1,0:T(8,128)}, u32[]{:S(2)}) copy-start(f32[8,2048]{1,0:T(8,128)} %user_ref.5) | copy-start | bytes 196612
  60.0 10.8 %collective-permute-start = (bf16[16,8,2048]{2,1,0:T(8,128)(2,1)S(1)}, bf16[16,8,2048]{2,1,0:T(8,128)(2,1)S(1)}, u32[]{:S(2)}, u32[]{:S(2)}) collective-permute-start(bf16[16,8,2048]{2,1,0:T(8,128)(2,1)S(1)} %get-tuple-element.23), channel_id=1, source_target_pairs={{0,1},{1,0},{2,3},{3,2},{4,5},{5,4},{6,7},{7,6},{8,9},{9,8},{10,11... | collective-permute-start | bytes 1572872 | tf_op jit(solution)/shard_map/ppermute | solution.py:300
  71.6 12.2 %all-to-all-start.1 = ((bf16[16,8,2048]{2,1,0:T(8,128)(2,1)}), bf16[16,8,2048]{2,1,0:T(8,128)(2,1)S(1)}, u32[]{:S(2)}, u32[]{:S(2)}) async-start(bf16[16,8,2048]{2,1,0:T(8,128)(2,1)} %halves.1), calls=%async_computation.1 | async-start | bytes 1048576 | tf_op jit(solution)/shard_map/all_to_all | solution.py:291
